TPU v7x, 32 devices: a whole 2x2x4 slice. The times are simulated.
32 devices in a mesh: gx: 8 (over y, x, core), gy: 4 (over z).
Axes of the slice: x: 2, y: 2, z: 4, core: 2. Of those that a mesh axis runs over, the one named last changes fastest.
Arguments:
- point_feats: bfloat16 [262144, 128], P(('gx', 'gy')), may hold values from -6 to 6
- point_tile: int32 [262144, 1], P(('gx', 'gy')), may hold values from 0 to 31; in each aligned block of 8192 rows (0 to 8191, 8192 to 16383, ...) at most 320 rows name the same one
- point_cell: int32 [262144], P(('gx', 'gy')), may hold values from 0 to 4095
- point_count: int32 [32], P(('gx', 'gy')), may hold values from 6144 to 8192, as said below
- conv_weight: bfloat16 [3, 3, 128, 128], replicated, may hold values from -0.1875 to 0.1875
- conv_bias: float32 [128], replicated, may hold values from -3 to 3
Outputs:
- bev_map: bfloat16 [128, 1024, 128], P('gx', 'gy')
- conv_out: bfloat16 [128, 1024, 128], P('gx', 'gy')
Inputs may be any that keep to these rules, and one draw needn't show every extreme that they name: `point_tile`: among the 8192 rows of one device no tile is named by more than 320 rows, a bound that some block reaches. `point_count`: only slots below a device's count are live; some device has all 8192 slots live.
All inputs are finite; a program needn't handle non-finite values.
Results may differ from a plain program's by a relative error of at most 0.0045.
Values may be sent and summed in bfloat16 or wider, within the bound.
A program may use at most 64 MiB of HBM per device.

v0:
```python
import functools

import jax
import jax.numpy as jnp
from jax import lax
from jax.experimental import pallas as pl
from jax.experimental.pallas import tpu as pltpu
from jax.sharding import PartitionSpec as P

COLS_DEV = 256
ROWS_DEV = 16
CELLS = ROWS_DEV * COLS_DEV


MESH = pl.DeviceIdType.MESH
GROUP = 4
CHUNK = 1024
NEIGHBOURS = [(dx, dy) for dx in (-1, 0, 1) for dy in (-1, 0, 1) if (dx, dy) != (0, 0)]


def map_kernel(
    size_gx,
    size_gy,
    feats,
    keys,
    taps,
    bias,
    bev,
    conv,
    weight,
    slots,
    tiles,
    meta,
    send_feats,
    send_cells,
    got_feats,
    got_cells,
    acc,
    pad,
    edges,
    sides,
    flat,
    send_f,
    recv_f,
    send_c,
    recv_c,
    own,
    send_h,
    recv_h,
):
    devices = size_gx * size_gy
    capacity = send_feats.shape[1]
    gx, gy = lax.axis_index("gx"), lax.axis_index("gy")
    me = gx * size_gy + gy

    for r in (0, ROWS_DEV + 1):
        pad[r] = jnp.zeros_like(pad[r])
    sides[...] = jnp.zeros_like(sides)

    barrier = pltpu.get_barrier_semaphore()

    @pl.loop(1, devices)
    def _(k):
        other = lax.rem(me + k, devices)
        pl.semaphore_signal(
            barrier, inc=1, device_id=(other // size_gy, lax.rem(other, size_gy)), device_id_type=MESH
        )

    chunks = keys.shape[0]
    stride = got_feats.shape[1]

    for a in range(3):
        for b in range(3):
            weight[a * 128 : (a + 1) * 128, b * 128 : (b + 1) * 128] = taps[a, b]
    inner = 256
    upper = lax.broadcasted_iota(jnp.int32, (inner, inner), 0) <= lax.broadcasted_iota(
        jnp.int32, (inner, inner), 1
    )
    upper = jnp.where(upper, 1.0, 0.0).astype(jnp.bfloat16)
    names = lax.broadcasted_iota(jnp.int32, (devices, inner), 0)

    def prepare(c, before):
        target = jnp.right_shift(keys[c].astype(jnp.int32), 12)
        found = []
        for at in range(0, CHUNK, inner):
            hits = jnp.where(names == target[:, at : at + inner], 1.0, 0.0)
            ranks = jnp.dot(hits.astype(jnp.bfloat16), upper, preferred_element_type=jnp.float32)
            found.append(jnp.sum(hits * (ranks + before), axis=0, keepdims=True) - 1.0)
            before = before + jnp.sum(hits, axis=1, keepdims=True)
        place = jnp.concatenate(found, axis=1).astype(jnp.int32)
        rows = pl.ds(pl.multiple_of(c * CHUNK, CHUNK), CHUNK)
        ids = lax.broadcasted_iota(jnp.int32, (capacity, CHUNK), 0)
        slots[c] = jnp.where(ids == place, 1.0, 0.0).astype(jnp.bfloat16)
        key = jnp.transpose(jnp.broadcast_to(keys[c], (128, CHUNK))).astype(jnp.int32)
        tile = jnp.right_shift(key, 12)
        tiles[rows, :] = tile.astype(jnp.float32).astype(jnp.bfloat16)
        hit = tile == lax.broadcasted_iota(jnp.int32, (CHUNK, 128), 1)
        row = (jnp.right_shift(key, 8) & (ROWS_DEV - 1)) + 1
        col = key & (COLS_DEV - 1)
        for at, part in ((0, row), (128, col)):
            part = jnp.where(hit, part, 0).astype(jnp.float32)
            meta[rows, at : at + 128] = part.astype(jnp.bfloat16)
        return before

    lax.fori_loop(0, chunks, prepare, jnp.zeros((devices, inner), jnp.float32))

    def packed(operand):
        total = None
        for c in range(chunks):
            part = jnp.dot(slots[c], operand(c), preferred_element_type=jnp.float32)
            total = part if total is None else total + part
        return total

    found = packed(lambda c: meta[c * CHUNK : (c + 1) * CHUNK, :])
    found = found[:, :128] * 256.0 + found[:, 128:]
    if stride > capacity:
        found = jnp.concatenate([found, jnp.zeros((stride - capacity, 128), jnp.float32)], axis=0)
    found = jnp.transpose(found)
    for t in range(devices):
        send_cells[t] = found[t : t + 1, :]

    pl.semaphore_wait(barrier, devices - 1)

    def copies(source, owner, target):
        where = dict(
            device_id=(target // size_gy, lax.rem(target, size_gy)), device_id_type=MESH
        )
        return (
            pltpu.make_async_remote_copy(
                send_cells.at[source], got_cells.at[owner],
                send_c.at[source], recv_c.at[owner], **where,
            ),
            pltpu.make_async_remote_copy(
                send_feats.at[source], got_feats.at[owner, pl.ds(0, capacity)],
                send_f.at[source], recv_f.at[owner], **where,
            ),
        )

    mine = (
        pltpu.make_async_copy(send_cells.at[me], got_cells.at[me], own.at[0]),
        pltpu.make_async_copy(
            send_feats.at[me], got_feats.at[me, pl.ds(0, capacity)], own.at[1]
        ),
    )
    pairs = devices // 2
    half = me // 2

    def offset(q):
        return lax.rem(2 * q + 1, pairs) - q // (pairs // 2)

    def send(q):
        pair = lax.rem(half + offset(q), pairs)
        for k in range(2):
            target = pair * 2 + k

            @pl.when(target != me)
            def _():
                for copy in copies(target, me, target):
                    copy.start()

            @pl.when(target == me)
            def _():
                for copy in mine:
                    copy.start()

    @pl.loop(0, pairs)
    def _(q):
        pair = lax.rem(half + offset(q), pairs)
        names = [(pair * 2 + k).astype(jnp.float32).astype(jnp.bfloat16) for k in range(2)]

        def masked(c):
            rows = slice(c * CHUNK, (c + 1) * CHUNK)
            values, tile = feats[rows, :], tiles[rows, :]
            zero = jnp.zeros_like(values)
            return jnp.concatenate([jnp.where(tile == n, values, zero) for n in names], axis=1)

        block = packed(masked).astype(jnp.bfloat16)
        for k in range(2):
            send_feats[pair * 2 + k] = block[:, k * 128 : (k + 1) * 128]

        @pl.when(q > 0)
        def _():
            send(q - 1)

    send(pairs - 1)
    acc[...] = jnp.zeros_like(acc)

    @pl.loop(0, devices // GROUP)
    def _(g):
        owners = []
        for j in range(GROUP // 2):
            q = lax.rem(g * (GROUP // 2) + j + pairs // 2, pairs)
            pair = lax.rem(half + pairs - offset(q), pairs)
            owners += [pair * 2, pair * 2 + 1]
        for owner in owners:

            @pl.when(owner != me)
            def _():
                for copy in copies(owner, owner, owner):
                    copy.wait_recv()

            @pl.when(owner == me)
            def _():
                for copy in mine:
                    copy.wait()

        cells = jnp.concatenate([got_cells[owner] for owner in owners], axis=1).astype(jnp.int32)
        values = jnp.concatenate([got_feats[owner] for owner in owners], axis=0)
        length = cells.shape[1]
        row = (jnp.right_shift(cells, 8) - 1).astype(jnp.float32)
        row = jnp.transpose(jnp.broadcast_to(row, (128, length))).astype(jnp.bfloat16)
        col = cells & (COLS_DEV - 1)
        ids = lax.broadcasted_iota(jnp.int32, (COLS_DEV, length), 0)
        onehot = jnp.where(ids == col, 1.0, 0.0).astype(jnp.bfloat16)
        zero = jnp.zeros_like(values)
        for r in range(0, ROWS_DEV, 2):
            masked = jnp.concatenate(
                [jnp.where(row == jnp.bfloat16(r + k), values, zero) for k in range(2)], axis=1
            )
            part = jnp.dot(onehot, masked, preferred_element_type=jnp.float32)
            acc[:, r * 128 : (r + 2) * 128] += part

    for r in range(ROWS_DEV):
        for side, c in ((0, 0), (1, COLS_DEV - 1)):
            edge = acc[c : c + 1, r * 128 : (r + 1) * 128]
            edges[side, r] = edge.astype(jnp.bfloat16).astype(jnp.float32)
    for r in range(ROWS_DEV):
        cells = acc[:, r * 128 : (r + 1) * 128].astype(jnp.bfloat16)
        pad[r + 1] = cells
        bev[r] = cells

    def inside(x, y):
        return (x >= 0) & (x < size_gx) & (y >= 0) & (y < size_gy)

    def halo(i):
        dx, dy = NEIGHBOURS[i]
        if dy == 0:
            src, dst = (pad.at[1], pad.at[ROWS_DEV + 1]) if dx < 0 else (pad.at[ROWS_DEV], pad.at[0])
        else:
            from_side, to_side = (0, 1) if dy < 0 else (1, 0)
            if dx == 0:
                src = edges.at[from_side]
                dst = sides.at[to_side, pl.ds(1, ROWS_DEV)]
            else:
                at = 0 if dx < 0 else ROWS_DEV - 1
                src = edges.at[from_side, pl.ds(at, 1)]
                dst = sides.at[to_side, pl.ds(ROWS_DEV + 1 if dx < 0 else 0, 1)]
        return pltpu.make_async_remote_copy(
            src, dst, send_h.at[i], recv_h.at[i], device_id=(gx + dx, gy + dy), device_id_type=MESH
        )

    for i, (dx, dy) in enumerate(NEIGHBOURS):

        @pl.when(inside(gx + dx, gy + dy))
        def _():
            halo(i).start()

    for i, (dx, dy) in enumerate(NEIGHBOURS):

        @pl.when(inside(gx - dx, gy - dy))
        def _():
            halo(i).wait_recv()

    side_sums = []
    for side in range(2):
        for r in range(ROWS_DEV + 2):
            flat[r : r + 1, :] = sides[side, r]
        near = jnp.concatenate([flat[a : a + ROWS_DEV, :] for a in range(3)], axis=1)
        taps = weight[:, :128] if side == 0 else weight[:, 256:]
        side_sums.append(
            jnp.dot(near.astype(jnp.bfloat16), taps, preferred_element_type=jnp.float32)
        )
    for side in range(2):
        flat[side * ROWS_DEV : (side + 1) * ROWS_DEV, :] = side_sums[side]
    place = lax.broadcasted_iota(jnp.int32, (COLS_DEV, 128), 0)

    @pl.loop(0, ROWS_DEV)
    def _(r):
        near = jnp.concatenate([pad[r + a] for a in range(3)], axis=1)
        sums = jnp.dot(near, weight[...], preferred_element_type=jnp.float32)
        left = jnp.where(place == 0, flat[pl.ds(r, 1), :], pltpu.roll(sums[:, :128], 1, 0))
        right = jnp.where(
            place == COLS_DEV - 1,
            flat[pl.ds(r + ROWS_DEV, 1), :],
            pltpu.roll(sums[:, 256:], COLS_DEV - 1, 0),
        )
        total = sums[:, 128:256] + left + right + bias[...]
        conv[r] = jnp.maximum(total, 0.0).astype(jnp.bfloat16)

    for i, (dx, dy) in enumerate(NEIGHBOURS):

        @pl.when(inside(gx + dx, gy + dy))
        def _():
            halo(i).wait_send()

    @pl.loop(1, devices)
    def _(k):
        other = lax.rem(me + k, devices)
        for copy in copies(other, me, other):
            copy.wait_send()


def make_map(feats, keys, weight, bias, size_gx, size_gy, capacity):
    devices = size_gx * size_gy
    points, channels = feats.shape
    stride = -(-capacity // 128) * 128
    vmem = pl.BlockSpec(memory_space=pltpu.VMEM)
    shape = jax.ShapeDtypeStruct((ROWS_DEV, COLS_DEV, channels), jnp.bfloat16)
    dma = pltpu.SemaphoreType.DMA
    return pl.pallas_call(
        functools.partial(map_kernel, size_gx, size_gy),
        out_shape=(shape, shape),
        in_specs=[vmem] * 4,
        out_specs=(vmem, vmem),
        scratch_shapes=[
            pltpu.VMEM((3 * channels, 3 * channels), jnp.bfloat16),
            pltpu.VMEM((points // CHUNK, capacity, CHUNK), jnp.bfloat16),
            pltpu.VMEM((points, 128), jnp.bfloat16),
            pltpu.VMEM((points, 256), jnp.bfloat16),
            pltpu.VMEM((devices, capacity, channels), jnp.bfloat16),
            pltpu.VMEM((devices, 1, stride), jnp.float32),
            pltpu.VMEM((devices, stride, channels), jnp.bfloat16),
            pltpu.VMEM((devices, 1, stride), jnp.float32),
            pltpu.VMEM((COLS_DEV, ROWS_DEV * channels), jnp.float32),
            pltpu.VMEM((ROWS_DEV + 2, COLS_DEV, channels), jnp.bfloat16),
            pltpu.VMEM((2, ROWS_DEV, 1, channels), jnp.float32),
            pltpu.VMEM((2, ROWS_DEV + 2, 1, channels), jnp.float32),
            pltpu.VMEM((2 * ROWS_DEV, channels), jnp.float32),
            dma((devices,)),
            dma((devices,)),
            dma((devices,)),
            dma((devices,)),
            dma((2,)),
            dma((len(NEIGHBOURS),)),
            dma((len(NEIGHBOURS),)),
        ],
        compiler_params=pltpu.CompilerParams(
            collective_id=0, has_side_effects=True, vmem_limit_bytes=56 * 1024 * 1024
        ),
        name="make_map",
    )(feats, keys, weight, bias)


def shards(point_feats, point_tile, point_cell, point_count, conv_weight, conv_bias):
    size_gx = lax.axis_size("gx")
    size_gy = lax.axis_size("gy")
    devices = size_gx * size_gy
    points = point_feats.shape[0]
    channels = point_feats.shape[1]
    capacity = 5 * points // (4 * devices)
    target = point_tile[:, 0]
    live = jnp.arange(points, dtype=jnp.int32) < point_count[0]
    keys = jnp.where(live, target, devices) * CELLS + point_cell
    return make_map(
        point_feats,
        keys.astype(jnp.float32).reshape(-1, 1, CHUNK),
        conv_weight,
        conv_bias.reshape(1, channels),
        size_gx,
        size_gy,
        capacity,
    )


def solution(mesh):
    in_specs = (
        P(("gx", "gy"), None),
        P(("gx", "gy"), None),
        P(("gx", "gy")),
        P(("gx", "gy")),
        P(),
        P(),
    )
    out_specs = (P("gx", "gy", None), P("gx", "gy", None))
    return jax.shard_map(shards, mesh=mesh, in_specs=in_specs, out_specs=out_specs, check_vma=False)
```

profile of v0, /device:TPU:0, one launch (start us, length us, event | category | flops | bytes accessed | tf_op | source)
XLA Modules:
  0.0 92.7 jit_solution(952914596395187928)
XLA Ops:
  1.3 1.4 %add_convert_fusion = f32[8192]{0:T(1024)} fusion(s32[8192]{0:T(1024)} %param.8, s32[8192]{0:T(1024)} %bitcast.6, s32[]{:T(128)} %bitcast.4), kind=kLoop, calls=%fused_computation | loop fusion | flops 40960 | bytes 98308 | tf_op jit(solution)/shard_map/convert_element_type | solution.py:356
  2.7 86.7 %make_map.1 = (bf16[16,256,128]{2,1,0:T(8,128)(2,1)}, bf16[16,256,128]{2,1,0:T(8,128)(2,1)}) custom-call(bf16[8192,128]{1,0:T(8,128)(2,1)} %feats.1, f32[8,1,1024]{2,1,0:T(1,128)} %bitcast.5, bf16[3,3,128,128]{3,2,1,0:T(8,128)(2,1)} %taps.1, f32[1,128]{1,0:T(1,128)} %bitcast.7), custom_call_target="tpu_custom_call" | custom-call | tf_op jit(solution)/shard_map/make_map/pallas_call | solution.py:310
  89.3 0.0 copy-start
  89.3 2.4 %copy.11 = bf16[16,256,128]{2,1,0:T(8,128)(2,1)} copy(bf16[16,256,128]{2,1,0:T(8,128)(2,1)} %get-tuple-element.4) | data formatting | bytes 2097152
  91.7 0.0 copy-done
  91.7 1.0 %copy.12 = bf16[16,256,128]{2,1,0:T(8,128)(2,1)} copy(bf16[16,256,128]{2,1,0:T(8,128)(2,1)S(1)} %copy-done) | data formatting | bytes 2097152
Async XLA Ops:
  89.3 2.4 %copy-start = (bf16[16,256,128]{2,1,0:T(8,128)(2,1)S(1)}, bf16[16,256,128]{2,1,0:T(8,128)(2,1)}, u32[]{:S(2)}) copy-start(bf16[16,256,128]{2,1,0:T(8,128)(2,1)} %get-tuple-element.5) | copy-start | bytes 3145732
where the time goes:
time: 93.1 us; the launch traced here: 92.7 us
  Pallas kernels  86.7 us (93%)
  local copies, waits for them, and re-layouts  3.36 us (4%)
  other arithmetic  1.4 us (2%)
  between operations  1.29 us (1%)
    pallas_call x1, Pallas kernels, make_map(): pl.pallas_call(functools.partial(map_kernel, size_gx, size_gy), out_shape...  86.7 us
    unnamed x4, local copies, waits for them, and re-layouts  3.36 us

commit v1 on v0

v1 whole, which is shorter than its diff:
```python
import functools

import jax
import jax.numpy as jnp
from jax import lax
from jax.experimental import pallas as pl
from jax.experimental.pallas import tpu as pltpu
from jax.sharding import PartitionSpec as P

COLS_DEV = 256
ROWS_DEV = 16
CELLS = ROWS_DEV * COLS_DEV


MESH = pl.DeviceIdType.MESH
GROUP = 4
CHUNK = 1024
NEIGHBOURS = [(dx, dy) for dx in (-1, 0, 1) for dy in (-1, 0, 1) if (dx, dy) != (0, 0)]


def map_kernel(
    size_gx,
    size_gy,
    count,
    source,
    named,
    cell,
    taps,
    bias,
    bev,
    conv,
    weight,
    feats,
    slots,
    tiles,
    meta,
    send_feats,
    send_cells,
    got_feats,
    got_cells,
    acc,
    pad,
    edges,
    sides,
    ends,
    flat,
    fetch,
    send_f,
    recv_f,
    send_c,
    recv_c,
    own,
    send_h,
    recv_h,
):
    devices = size_gx * size_gy
    capacity = send_feats.shape[1]
    gx, gy = lax.axis_index("gx"), lax.axis_index("gy")
    me = gx * size_gy + gy

    barrier = pltpu.get_barrier_semaphore()

    @pl.loop(1, devices)
    def _(k):
        other = lax.rem(me + k, devices)
        pl.semaphore_signal(
            barrier, inc=1, device_id=(other // size_gy, lax.rem(other, size_gy)), device_id_type=MESH
        )

    load = pltpu.make_async_copy(source, feats, fetch.at[0])
    load.start()

    for r in (0, ROWS_DEV + 1):
        pad[r] = jnp.zeros_like(pad[r])
    sides[...] = jnp.zeros_like(sides)

    chunks = named.shape[0]

    inner = 256
    upper = lax.broadcasted_iota(jnp.int32, (inner, inner), 0) <= lax.broadcasted_iota(
        jnp.int32, (inner, inner), 1
    )
    upper = jnp.where(upper, 1.0, 0.0).astype(jnp.bfloat16)
    names = lax.broadcasted_iota(jnp.int32, (devices, inner), 0)

    def prepare(c, before):
        slot = lax.broadcasted_iota(jnp.int32, (1, CHUNK), 1) + c * CHUNK
        target = jnp.where(slot < count[0], named[c], devices)
        hits = jnp.concatenate(
            [jnp.where(names == target[:, at : at + inner], 1.0, 0.0) for at in range(0, CHUNK, inner)],
            axis=0,
        )
        ranks = jnp.dot(hits.astype(jnp.bfloat16), upper, preferred_element_type=jnp.float32)
        found = []
        for at in range(0, CHUNK // inner * devices, devices):
            hit, rank = hits[at : at + devices], ranks[at : at + devices]
            found.append(jnp.sum(hit * (rank + before), axis=0, keepdims=True) - 1.0)
            before = before + rank[:, inner - 1 : inner]
        place = jnp.concatenate(found, axis=1).astype(jnp.int32)
        rows = pl.ds(pl.multiple_of(c * CHUNK, CHUNK), CHUNK)
        ids = lax.broadcasted_iota(jnp.int32, (capacity, CHUNK), 0)
        slots[c] = jnp.where(ids == place, 1.0, 0.0).astype(jnp.bfloat16)
        key = (target * CELLS + cell[c]).astype(jnp.float32)
        key = jnp.transpose(jnp.broadcast_to(key, (128, CHUNK))).astype(jnp.int32)
        tile = jnp.right_shift(key, 12)
        tiles[rows, :] = tile.astype(jnp.float32).astype(jnp.bfloat16)
        hit = tile == lax.broadcasted_iota(jnp.int32, (CHUNK, 128), 1)
        row = (jnp.right_shift(key, 8) & (ROWS_DEV - 1)) + 1
        col = key & (COLS_DEV - 1)
        for at, part in ((0, row), (128, col)):
            part = jnp.where(hit, part, 0).astype(jnp.float32)
            meta[rows, at : at + 128] = part.astype(jnp.bfloat16)
        return before

    lax.fori_loop(0, chunks, prepare, jnp.zeros((devices, inner), jnp.float32))

    def packed(operand):
        total = None
        for c in range(chunks):
            part = jnp.dot(slots[c], operand(c), preferred_element_type=jnp.float32)
            total = part if total is None else total + part
        return total

    def copies(source, owner, target):
        where = dict(
            device_id=(target // size_gy, lax.rem(target, size_gy)), device_id_type=MESH
        )
        return (
            pltpu.make_async_remote_copy(
                send_cells.at[source], got_cells.at[owner],
                send_c.at[source], recv_c.at[owner], **where,
            ),
            pltpu.make_async_remote_copy(
                send_feats.at[source], got_feats.at[owner], send_f.at[source], recv_f.at[owner], **where
            ),
        )

    mine = (
        pltpu.make_async_copy(send_cells.at[me], got_cells.at[me], own.at[0]),
        pltpu.make_async_copy(send_feats.at[me], got_feats.at[me], own.at[1]),
    )
    pairs = devices // 2
    half = me // 2

    def offset(q):
        return lax.rem(2 * q + 1, pairs) - q // (pairs // 2)

    def pack(q):
        pair = lax.rem(half + offset(q), pairs)
        names = [(pair * 2 + k).astype(jnp.float32).astype(jnp.bfloat16) for k in range(2)]

        def masked(c):
            rows = slice(c * CHUNK, (c + 1) * CHUNK)
            values, tile = feats[rows, :], tiles[rows, :]
            zero = jnp.zeros_like(values)
            return jnp.concatenate([jnp.where(tile == n, values, zero) for n in names], axis=1)

        block = packed(masked).astype(jnp.bfloat16)
        for k in range(2):
            send_feats[pair * 2 + k] = block[:, k * 128 : (k + 1) * 128]

    def send(q):
        pair = lax.rem(half + offset(q), pairs)
        for k in range(2):
            target = pair * 2 + k

            @pl.when(target != me)
            def _():
                for copy in copies(target, me, target):
                    copy.start()

            @pl.when(target == me)
            def _():
                for copy in mine:
                    copy.start()

    load.wait()
    pack(jnp.int32(0))

    found = packed(lambda c: meta[c * CHUNK : (c + 1) * CHUNK, :])
    found = found[:, :128] * 256.0 + found[:, 128:]
    if send_cells.shape[2] > capacity:
        found = jnp.concatenate(
            [found, jnp.zeros((send_cells.shape[2] - capacity, 128), jnp.float32)], axis=0
        )
    found = jnp.transpose(found)
    for t in range(devices):
        send_cells[t] = found[t : t + 1, :]

    pl.semaphore_wait(barrier, devices - 1)
    send(jnp.int32(0))

    @pl.loop(1, pairs)
    def _(q):
        pack(q)

        @pl.when(q > 1)
        def _():
            send(q - 1)

    for a in range(3):
        for b in range(3):
            weight[a * 128 : (a + 1) * 128, b * 128 : (b + 1) * 128] = taps[a, b]
    send(jnp.int32(pairs - 1))
    acc[...] = jnp.zeros_like(acc)

    def receive(positions):
        owners = []
        for j in positions:
            q = lax.rem(j + pairs // 2, pairs)
            pair = lax.rem(half + pairs - offset(q), pairs)
            owners += [pair * 2, pair * 2 + 1]
        for owner in owners:

            @pl.when(owner != me)
            def _():
                for copy in copies(owner, owner, owner):
                    copy.wait_recv()

            @pl.when(owner == me)
            def _():
                for copy in mine:
                    copy.wait()

        cells = [got_cells[owner] for owner in owners]
        values = jnp.concatenate([got_feats[owner] for owner in owners], axis=0)
        row, onehot = [], []
        for part in cells:
            part = part.astype(jnp.int32)
            at = (jnp.right_shift(part, 8) - 1).astype(jnp.float32)
            at = jnp.transpose(jnp.broadcast_to(at, (128, part.shape[1])))
            row.append(at[:capacity].astype(jnp.bfloat16))
            part = part[:, :capacity]
            onehot.append(part & (COLS_DEV - 1))
        row = jnp.concatenate(row, axis=0)
        col = jnp.concatenate(onehot, axis=1)
        ids = lax.broadcasted_iota(jnp.int32, (COLS_DEV, col.shape[1]), 0)
        onehot = jnp.where(ids == col, 1.0, 0.0).astype(jnp.bfloat16)
        zero = jnp.zeros_like(values)

        def added(rows):
            masked = jnp.concatenate(
                [jnp.where(row == jnp.bfloat16(r), values, zero) for r in rows], axis=1
            )
            return jnp.dot(onehot, masked, preferred_element_type=jnp.float32)

        return added

    group = GROUP // 2

    @pl.loop(0, pairs // group - 1)
    def _(g):
        added = receive([g * group + j for j in range(group)])
        for r in range(0, ROWS_DEV, 2):
            acc[:, r * 128 : (r + 2) * 128] += added((r, r + 1))

    for j in range(pairs - group, pairs - 1):
        added = receive([jnp.int32(j)])
        for r in range(0, ROWS_DEV, 2):
            acc[:, r * 128 : (r + 2) * 128] += added((r, r + 1))

    def inside(x, y):
        return (x >= 0) & (x < size_gx) & (y >= 0) & (y < size_gy)

    def halo(i):
        dx, dy = NEIGHBOURS[i]
        if dy == 0:
            src, dst = (pad.at[1], pad.at[ROWS_DEV + 1]) if dx < 0 else (pad.at[ROWS_DEV], pad.at[0])
        else:
            from_side, to_side = (0, 1) if dy < 0 else (1, 0)
            if dx == 0:
                src = edges.at[from_side]
                dst = sides.at[to_side, pl.ds(1, ROWS_DEV)]
            else:
                at = 0 if dx < 0 else ROWS_DEV - 1
                src = edges.at[from_side, pl.ds(at, 1)]
                dst = sides.at[to_side, pl.ds(ROWS_DEV + 1 if dx < 0 else 0, 1)]
        return pltpu.make_async_remote_copy(
            src, dst, send_h.at[i], recv_h.at[i], device_id=(gx + dx, gy + dy), device_id_type=MESH
        )

    def start(which):
        for i, (dx, dy) in enumerate(NEIGHBOURS):
            if which(dx, dy):

                @pl.when(inside(gx + dx, gy + dy))
                def _():
                    halo(i).start()

    added = receive([jnp.int32(pairs - 1)])
    order = [(0, ROWS_DEV - 1)] + [(r, r + 1) for r in range(1, ROWS_DEV - 1, 2)]
    for step, rows in enumerate(order):
        part = added(rows)
        for k, r in enumerate(rows):
            total = acc[:, r * 128 : (r + 1) * 128] + part[:, k * 128 : (k + 1) * 128]
            cells = total.astype(jnp.bfloat16)
            pad[r + 1] = cells
            bev[r] = cells
            for side, c in ((0, 0), (1, COLS_DEV - 1)):
                edges[side, r] = total[c : c + 1].astype(jnp.bfloat16).astype(jnp.float32)
        if step == 1:
            start(lambda dx, dy: dy == 0)
        if step == 2:
            start(lambda dx, dy: dx != 0 and dy != 0)

    place = lax.broadcasted_iota(jnp.int32, (COLS_DEV, 128), 0)

    def sums_of(r):
        near = jnp.concatenate([pad[r + a] for a in range(3)], axis=1)
        sums = jnp.dot(near, weight[...], preferred_element_type=jnp.float32)
        left = jnp.where(place == 0, 0.0, pltpu.roll(sums[:, :128], 1, 0))
        right = jnp.where(place == COLS_DEV - 1, 0.0, pltpu.roll(sums[:, 256:], COLS_DEV - 1, 0))
        total = sums[:, 128:256] + left + right + bias[...]
        for side, c in ((0, 0), (1, COLS_DEV - 1)):
            ends[side, r] = total[c : c + 1]
        conv[r] = jnp.maximum(total, 0.0).astype(jnp.bfloat16)

    start(lambda dx, dy: dx == 0)

    @pl.loop(1, ROWS_DEV - 1)
    def _(r):
        sums_of(r)

    for i, (dx, dy) in enumerate(NEIGHBOURS):

        @pl.when(inside(gx - dx, gy - dy))
        def _():
            halo(i).wait_recv()

    for r in (0, ROWS_DEV - 1):
        sums_of(r)

    side_sums = []
    for side in range(2):
        for r in range(ROWS_DEV + 2):
            flat[r : r + 1, :] = sides[side, r]
        near = jnp.concatenate([flat[a : a + ROWS_DEV, :] for a in range(3)], axis=1)
        part = weight[:, :128] if side == 0 else weight[:, 256:]
        side_sums.append(
            jnp.dot(near.astype(jnp.bfloat16), part, preferred_element_type=jnp.float32)
        )
    lines = 16
    place = lax.broadcasted_iota(jnp.int32, (lines, 128), 0)
    for side, c in ((0, 0), (1, COLS_DEV - 1)):
        rows = pl.ds(c // lines * lines, lines)
        for r in range(ROWS_DEV):
            total = jnp.maximum(ends[side, r] + side_sums[side][r : r + 1], 0.0)
            kept = conv[r, rows, :].astype(jnp.float32)
            conv[r, rows, :] = jnp.where(place == c % lines, total, kept).astype(jnp.bfloat16)

    for i, (dx, dy) in enumerate(NEIGHBOURS):

        @pl.when(inside(gx + dx, gy + dy))
        def _():
            halo(i).wait_send()

    @pl.loop(1, devices)
    def _(k):
        other = lax.rem(me + k, devices)
        for copy in copies(other, me, other):
            copy.wait_send()


def make_map(count, feats, named, cell, weight, bias, size_gx, size_gy, capacity):
    devices = size_gx * size_gy
    points, channels = feats.shape
    stride = -(-capacity // 128) * 128
    vmem = pl.BlockSpec(memory_space=pltpu.VMEM)
    shape = jax.ShapeDtypeStruct((ROWS_DEV, COLS_DEV, channels), jnp.bfloat16)
    dma = pltpu.SemaphoreType.DMA
    return pl.pallas_call(
        functools.partial(map_kernel, size_gx, size_gy),
        out_shape=(shape, shape),
        in_specs=[
            pl.BlockSpec(memory_space=pltpu.SMEM),
            pl.BlockSpec(memory_space=pltpu.HBM),
            vmem,
            vmem,
            vmem,
            vmem,
        ],
        out_specs=(vmem, vmem),
        scratch_shapes=[
            pltpu.VMEM((3 * channels, 3 * channels), jnp.bfloat16),
            pltpu.VMEM((points, channels), jnp.bfloat16),
            pltpu.VMEM((points // CHUNK, capacity, CHUNK), jnp.bfloat16),
            pltpu.VMEM((points, 128), jnp.bfloat16),
            pltpu.VMEM((points, 256), jnp.bfloat16),
            pltpu.VMEM((devices, capacity, channels), jnp.bfloat16),
            pltpu.VMEM((devices, 1, stride), jnp.float32),
            pltpu.VMEM((devices, capacity, channels), jnp.bfloat16),
            pltpu.VMEM((devices, 1, stride), jnp.float32),
            pltpu.VMEM((COLS_DEV, ROWS_DEV * channels), jnp.float32),
            pltpu.VMEM((ROWS_DEV + 2, COLS_DEV, channels), jnp.bfloat16),
            pltpu.VMEM((2, ROWS_DEV, 1, channels), jnp.float32),
            pltpu.VMEM((2, ROWS_DEV + 2, 1, channels), jnp.float32),
            pltpu.VMEM((2, ROWS_DEV, 1, channels), jnp.float32),
            pltpu.VMEM((2 * ROWS_DEV, channels), jnp.float32),
            dma((1,)),
            dma((devices,)),
            dma((devices,)),
            dma((devices,)),
            dma((devices,)),
            dma((2,)),
            dma((len(NEIGHBOURS),)),
            dma((len(NEIGHBOURS),)),
        ],
        compiler_params=pltpu.CompilerParams(
            collective_id=0, has_side_effects=True, vmem_limit_bytes=36 * 1024 * 1024
        ),
        name="make_map",
    )(count, feats, named, cell, weight, bias)


def shards(point_feats, point_tile, point_cell, point_count, conv_weight, conv_bias):
    size_gx = lax.axis_size("gx")
    size_gy = lax.axis_size("gy")
    devices = size_gx * size_gy
    points = point_feats.shape[0]
    channels = point_feats.shape[1]
    capacity = 5 * points // (4 * devices)
    return make_map(
        point_count,
        point_feats,
        point_tile.reshape(-1, 1, CHUNK),
        point_cell.reshape(-1, 1, CHUNK),
        conv_weight,
        conv_bias.reshape(1, channels),
        size_gx,
        size_gy,
        capacity,
    )


def solution(mesh):
    in_specs = (
        P(("gx", "gy"), None),
        P(("gx", "gy"), None),
        P(("gx", "gy")),
        P(("gx", "gy")),
        P(),
        P(),
    )
    out_specs = (P("gx", "gy", None), P("gx", "gy", None))
    return jax.shard_map(shards, mesh=mesh, in_specs=in_specs, out_specs=out_specs, check_vma=False)
```

time: 93.1 us -> 85.3 us (0.916)
  Pallas kernels: 86.7 us -> 77 us
  local copies, waits for them, and re-layouts: 3.36 us -> 6.66 us
  other arithmetic: 1.4 us -> 0 us
    pallas_call x1, Pallas kernels: 86.7 us -> 77 us  [make_map(): pl.pallas_call(functools.partial(map_kernel, size_gx, size_gy), out_shape...]
    unnamed x4 -> x12, local copies, waits for them, and re-layouts: 3.36 us -> 6.66 us
    convert_element_type x1 -> x0, other arithmetic: 1.4 us -> none  [shards(): keys.astype(jnp.float32).reshape(-1, 1, CHUNK)]
where the time goes in v1:
time: 85.3 us; the launch traced here: 85 us
  Pallas kernels  77 us (90%)
  local copies, waits for them, and re-layouts  6.66 us (8%)
  between operations  1.3 us (2%)
    pallas_call x1, Pallas kernels, make_map(): pl.pallas_call(functools.partial(map_kernel, size_gx, size_gy), out_shape...  77 us
    unnamed x12, local copies, waits for them, and re-layouts  6.66 us

profile of v1, /device:TPU:0, one launch (start us, length us, event | category | flops | bytes accessed | tf_op | source)
XLA Modules:
  0.0 85.0 jit_solution(10214267605657209867)
XLA Ops:
  1.3 0.0 copy-start
  1.3 1.6 %copy-done = bf16[8192,128]{1,0:T(8,128)(2,1)S(1)} copy-done((bf16[8192,128]{1,0:T(8,128)(2,1)S(1)}, bf16[8192,128]{1,0:T(8,128)(2,1)}, u32[]{:S(2)}) %copy-start) | copy-done | bytes 2097176
  2.9 0.0 copy-start.1
  2.9 1.0 %copy-done.1 = bf16[3,3,128,128]{3,2,1,0:T(8,128)(2,1)S(1)} copy-done((bf16[3,3,128,128]{3,2,1,0:T(8,128)(2,1)S(1)}, bf16[3,3,128,128]{3,2,1,0:T(8,128)(2,1)}, u32[]{:S(2)}) %copy-start.1) | copy-done | bytes 294936
  3.8 0.0 copy-start.2
  3.8 0.8 copy-done.2
  4.6 0.0 copy-start.3
  4.6 0.8 copy-done.3
  5.3 0.0 copy-start.4
  5.4 0.7 copy-done.4
  6.0 77.0 %make_map.1 = (bf16[16,256,128]{2,1,0:T(8,128)(2,1)S(1)}, bf16[16,256,128]{2,1,0:T(8,128)(2,1)S(1)}) custom-call(s32[1]{0:T(128)S(6)} %copy.10.count, bf16[8192,128]{1,0:T(8,128)(2,1)S(1)} %copy-done, s32[8,1,1024]{2,1,0:T(1,128)S(1)} %bitcast.3, s32[8,1,1024]{2,1,0:T(1,128)S(1)} %bitcast.4, bf16[3,3,128,128]{3,2,1,0:T(8,128)(2,1)S(1)} %copy-done.1, ...), custom_call_target="tpu_custom_call" | custom-call | tf_op jit(solution)/shard_map/make_map/pallas_call | solution.py:371
  83.0 1.0 %copy.11 = bf16[16,256,128]{2,1,0:T(8,128)(2,1)} copy(bf16[16,256,128]{2,1,0:T(8,128)(2,1)S(1)} %get-tuple-element.4) | data formatting | bytes 2097152
  84.0 1.0 %copy.12 = bf16[16,256,128]{2,1,0:T(8,128)(2,1)} copy(bf16[16,256,128]{2,1,0:T(8,128)(2,1)S(1)} %get-tuple-element.5) | data formatting | bytes 2097152
Async XLA Ops:
  1.3 1.6 %copy-start = (bf16[8192,128]{1,0:T(8,128)(2,1)S(1)}, bf16[8192,128]{1,0:T(8,128)(2,1)}, u32[]{:S(2)}) copy-start(bf16[8192,128]{1,0:T(8,128)(2,1)} %source.1) | copy-start | bytes 6291460
  2.9 1.0 %copy-start.1 = (bf16[3,3,128,128]{3,2,1,0:T(8,128)(2,1)S(1)}, bf16[3,3,128,128]{3,2,1,0:T(8,128)(2,1)}, u32[]{:S(2)}) copy-start(bf16[3,3,128,128]{3,2,1,0:T(8,128)(2,1)} %taps.1) | copy-start | bytes 884740
  3.8 0.8 copy-start.2
  4.6 0.8 copy-start.3
  5.3 0.7 copy-start.4

commit v2 on v1

--- a/solution.py
+++ b/solution.py
@@ -23,17 +23,20 @@
     size_gy,
     count,
     source,
-    named,
-    cell,
+    all_named,
+    all_cell,
     taps,
-    bias,
+    all_bias,
     bev,
     conv,
     weight,
     feats,
+    named,
+    cell,
+    bias,
     slots,
     tiles,
-    meta,
+    marks,
     send_feats,
     send_cells,
     got_feats,
@@ -67,8 +70,18 @@
             barrier, inc=1, device_id=(other // size_gy, lax.rem(other, size_gy)), device_id_type=MESH
         )
 
-    load = pltpu.make_async_copy(source, feats, fetch.at[0])
-    load.start()
+    points = (
+        pltpu.make_async_copy(all_named, named, fetch.at[0]),
+        pltpu.make_async_copy(all_cell, cell, fetch.at[1]),
+    )
+    load = pltpu.make_async_copy(source, feats, fetch.at[2])
+    later = [pltpu.make_async_copy(all_bias, bias, fetch.at[3])]
+    for a in range(3):
+        for b in range(3):
+            block = weight.at[pl.ds(a * 128, 128), pl.ds(b * 128, 128)]
+            later.append(pltpu.make_async_copy(taps.at[a, b], block, fetch.at[4 + a * 3 + b]))
+    for copy in (*points, load, *later):
+        copy.start()
 
     for r in (0, ROWS_DEV + 1):
         pad[r] = jnp.zeros_like(pad[r])
@@ -83,36 +96,45 @@
     upper = jnp.where(upper, 1.0, 0.0).astype(jnp.bfloat16)
     names = lax.broadcasted_iota(jnp.int32, (devices, inner), 0)
 
+    width = marks.shape[1] // 2
+    gap = jnp.zeros((width - devices, inner), jnp.float32)
+
+    middle = capacity // 2
+    assert middle < 256
+    ids = lax.broadcasted_iota(jnp.int32, (capacity, CHUNK), 0) - middle
+    ids = ids.astype(jnp.float32).astype(jnp.bfloat16)
+
     def prepare(c, before):
         slot = lax.broadcasted_iota(jnp.int32, (1, CHUNK), 1) + c * CHUNK
         target = jnp.where(slot < count[0], named[c], devices)
+        row = jnp.right_shift(cell[c], 8).astype(jnp.float32) * 256.0
+        col = (cell[c] & (COLS_DEV - 1)).astype(jnp.float32)
         hits = jnp.concatenate(
             [jnp.where(names == target[:, at : at + inner], 1.0, 0.0) for at in range(0, CHUNK, inner)],
             axis=0,
         )
         ranks = jnp.dot(hits.astype(jnp.bfloat16), upper, preferred_element_type=jnp.float32)
         found = []
-        for at in range(0, CHUNK // inner * devices, devices):
-            hit, rank = hits[at : at + devices], ranks[at : at + devices]
+        for k in range(CHUNK // inner):
+            hit, rank = (x[k * devices : (k + 1) * devices] for x in (hits, ranks))
             found.append(jnp.sum(hit * (rank + before), axis=0, keepdims=True) - 1.0)
             before = before + rank[:, inner - 1 : inner]
-        place = jnp.concatenate(found, axis=1).astype(jnp.int32)
-        rows = pl.ds(pl.multiple_of(c * CHUNK, CHUNK), CHUNK)
-        ids = lax.broadcasted_iota(jnp.int32, (capacity, CHUNK), 0)
-        slots[c] = jnp.where(ids == place, 1.0, 0.0).astype(jnp.bfloat16)
-        key = (target * CELLS + cell[c]).astype(jnp.float32)
-        key = jnp.transpose(jnp.broadcast_to(key, (128, CHUNK))).astype(jnp.int32)
-        tile = jnp.right_shift(key, 12)
-        tiles[rows, :] = tile.astype(jnp.float32).astype(jnp.bfloat16)
-        hit = tile == lax.broadcasted_iota(jnp.int32, (CHUNK, 128), 1)
-        row = (jnp.right_shift(key, 8) & (ROWS_DEV - 1)) + 1
-        col = key & (COLS_DEV - 1)
-        for at, part in ((0, row), (128, col)):
-            part = jnp.where(hit, part, 0).astype(jnp.float32)
-            meta[rows, at : at + 128] = part.astype(jnp.bfloat16)
+            at = slice(k * inner, (k + 1) * inner)
+            mark = [hit * row[:, at], gap, hit * col[:, at], gap]
+            mark = jnp.concatenate([m for m in mark if m.shape[0]], axis=0)
+            marks[c, :, at] = mark.astype(jnp.bfloat16)
+        place = (jnp.concatenate(found, axis=1) - middle).astype(jnp.bfloat16)
+        rows = pl.ds(c * CHUNK, CHUNK)
+        slots[c] = jnp.where(ids == place, jnp.bfloat16(1), jnp.bfloat16(0))
+        tile = jnp.transpose(jnp.broadcast_to(target.astype(jnp.float32), (128, CHUNK)))
+        tiles[rows, :] = tile.astype(jnp.bfloat16)
         return before
 
-    lax.fori_loop(0, chunks, prepare, jnp.zeros((devices, inner), jnp.float32))
+    for copy in points:
+        copy.wait()
+    before = jnp.zeros((devices, inner), jnp.float32)
+    for c in range(chunks):
+        before = prepare(c, before)
 
     def packed(operand):
         total = None
@@ -159,36 +181,41 @@
         for k in range(2):
             send_feats[pair * 2 + k] = block[:, k * 128 : (k + 1) * 128]
 
-    def send(q):
+    def send(q, parts=(0, 1)):
         pair = lax.rem(half + offset(q), pairs)
         for k in range(2):
             target = pair * 2 + k
 
             @pl.when(target != me)
             def _():
-                for copy in copies(target, me, target):
-                    copy.start()
+                for part in parts:
+                    copies(target, me, target)[part].start()
 
             @pl.when(target == me)
             def _():
-                for copy in mine:
-                    copy.start()
+                for part in parts:
+                    mine[part].start()
 
     load.wait()
     pack(jnp.int32(0))
 
-    found = packed(lambda c: meta[c * CHUNK : (c + 1) * CHUNK, :])
-    found = found[:, :128] * 256.0 + found[:, 128:]
+    found = None
+    for c in range(chunks):
+        part = lax.dot_general(
+            slots[c], marks[c], (((1,), (1,)), ((), ())), preferred_element_type=jnp.float32
+        )
+        found = part if found is None else found + part
     if send_cells.shape[2] > capacity:
-        found = jnp.concatenate(
-            [found, jnp.zeros((send_cells.shape[2] - capacity, 128), jnp.float32)], axis=0
-        )
+        extra = (send_cells.shape[2] - capacity, found.shape[1])
+        found = jnp.concatenate([found, jnp.zeros(extra, jnp.float32)], axis=0)
     found = jnp.transpose(found)
+    found = found[:devices] + found[width : width + devices]
     for t in range(devices):
         send_cells[t] = found[t : t + 1, :]
 
     pl.semaphore_wait(barrier, devices - 1)
     send(jnp.int32(0))
+
 
     @pl.loop(1, pairs)
     def _(q):
@@ -198,9 +225,8 @@
         def _():
             send(q - 1)
 
-    for a in range(3):
-        for b in range(3):
-            weight[a * 128 : (a + 1) * 128, b * 128 : (b + 1) * 128] = taps[a, b]
+    for copy in later:
+        copy.wait()
     send(jnp.int32(pairs - 1))
     acc[...] = jnp.zeros_like(acc)
 
@@ -210,32 +236,32 @@
             q = lax.rem(j + pairs // 2, pairs)
             pair = lax.rem(half + pairs - offset(q), pairs)
             owners += [pair * 2, pair * 2 + 1]
+
+        def arrived(part):
+            for owner in owners:
+
+                @pl.when(owner != me)
+                def _():
+                    copies(owner, owner, owner)[part].wait_recv()
+
+                @pl.when(owner == me)
+                def _():
+                    mine[part].wait()
+
+        arrived(0)
+        row, col = [], []
         for owner in owners:
-
-            @pl.when(owner != me)
-            def _():
-                for copy in copies(owner, owner, owner):
-                    copy.wait_recv()
-
-            @pl.when(owner == me)
-            def _():
-                for copy in mine:
-                    copy.wait()
-
-        cells = [got_cells[owner] for owner in owners]
-        values = jnp.concatenate([got_feats[owner] for owner in owners], axis=0)
-        row, onehot = [], []
-        for part in cells:
-            part = part.astype(jnp.int32)
-            at = (jnp.right_shift(part, 8) - 1).astype(jnp.float32)
+            part = got_cells[owner].astype(jnp.int32)
+            at = jnp.right_shift(part, 8).astype(jnp.float32)
             at = jnp.transpose(jnp.broadcast_to(at, (128, part.shape[1])))
             row.append(at[:capacity].astype(jnp.bfloat16))
-            part = part[:, :capacity]
-            onehot.append(part & (COLS_DEV - 1))
+            col.append(part[:, :capacity] & (COLS_DEV - 1))
         row = jnp.concatenate(row, axis=0)
-        col = jnp.concatenate(onehot, axis=1)
+        col = jnp.concatenate(col, axis=1)
         ids = lax.broadcasted_iota(jnp.int32, (COLS_DEV, col.shape[1]), 0)
         onehot = jnp.where(ids == col, 1.0, 0.0).astype(jnp.bfloat16)
+        arrived(1)
+        values = jnp.concatenate([got_feats[owner] for owner in owners], axis=0)
         zero = jnp.zeros_like(values)
 
         def added(rows):
@@ -366,26 +392,29 @@
     points, channels = feats.shape
     stride = -(-capacity // 128) * 128
     vmem = pl.BlockSpec(memory_space=pltpu.VMEM)
-    shape = jax.ShapeDtypeStruct((ROWS_DEV, COLS_DEV, channels), jnp.bfloat16)
+    shape = pltpu.VMEM((ROWS_DEV, COLS_DEV, channels), jnp.bfloat16)
+    hbm = [
+        pltpu.with_memory_space_constraint(a, pltpu.HBM)
+        for a in (feats, named, cell, weight, bias)
+    ]
     dma = pltpu.SemaphoreType.DMA
     return pl.pallas_call(
         functools.partial(map_kernel, size_gx, size_gy),
         out_shape=(shape, shape),
         in_specs=[
             pl.BlockSpec(memory_space=pltpu.SMEM),
-            pl.BlockSpec(memory_space=pltpu.HBM),
-            vmem,
-            vmem,
-            vmem,
-            vmem,
+            *[pl.BlockSpec(memory_space=pltpu.HBM)] * len(hbm),
         ],
         out_specs=(vmem, vmem),
         scratch_shapes=[
             pltpu.VMEM((3 * channels, 3 * channels), jnp.bfloat16),
             pltpu.VMEM((points, channels), jnp.bfloat16),
+            pltpu.VMEM(named.shape, jnp.int32),
+            pltpu.VMEM(cell.shape, jnp.int32),
+            pltpu.VMEM(bias.shape, jnp.float32),
             pltpu.VMEM((points // CHUNK, capacity, CHUNK), jnp.bfloat16),
             pltpu.VMEM((points, 128), jnp.bfloat16),
-            pltpu.VMEM((points, 256), jnp.bfloat16),
+            pltpu.VMEM((points // CHUNK, 2 * max(devices, 64), CHUNK), jnp.bfloat16),
             pltpu.VMEM((devices, capacity, channels), jnp.bfloat16),
             pltpu.VMEM((devices, 1, stride), jnp.float32),
             pltpu.VMEM((devices, capacity, channels), jnp.bfloat16),
@@ -396,7 +425,7 @@
             pltpu.VMEM((2, ROWS_DEV + 2, 1, channels), jnp.float32),
             pltpu.VMEM((2, ROWS_DEV, 1, channels), jnp.float32),
             pltpu.VMEM((2 * ROWS_DEV, channels), jnp.float32),
-            dma((1,)),
+            dma((13,)),
             dma((devices,)),
             dma((devices,)),
             dma((devices,)),
@@ -409,7 +438,7 @@
             collective_id=0, has_side_effects=True, vmem_limit_bytes=36 * 1024 * 1024
         ),
         name="make_map",
-    )(count, feats, named, cell, weight, bias)
+    )(count, *hbm)
 
 
 def shards(point_feats, point_tile, point_cell, point_count, conv_weight, conv_bias):

time: 85.3 us -> 77.9 us (0.913)
  local copies, waits for them, and re-layouts: 6.66 us -> 1.94 us
  Pallas kernels: 77 us -> 74.6 us
    unnamed x12 -> x2, local copies, waits for them, and re-layouts: 6.66 us -> 1.94 us
    pallas_call x1, Pallas kernels: 77 us -> 74.6 us  [make_map(): pl.pallas_call(functools.partial(map_kernel, size_gx, size_gy), out_shape...]
where the time goes in v2:
time: 77.9 us; the launch traced here: 77.8 us
  Pallas kernels  74.6 us (96%)
  local copies, waits for them, and re-layouts  1.94 us (2%)
  between operations  1.29 us (2%)
    pallas_call x1, Pallas kernels, make_map(): pl.pallas_call(functools.partial(map_kernel, size_gx, size_gy), out_shape...  74.6 us
    unnamed x2, local copies, waits for them, and re-layouts  1.94 us

profile of v2, /device:TPU:0, one launch (start us, length us, event | category | flops | bytes accessed | tf_op | source)
XLA Modules:
  0.0 77.8 jit_solution(14767712409174535730)
XLA Ops:
  1.3 74.6 %make_map.1 = (bf16[16,256,128]{2,1,0:T(8,128)(2,1)S(1)}, bf16[16,256,128]{2,1,0:T(8,128)(2,1)S(1)}) custom-call(s32[1]{0:T(128)S(6)} %copy.12.count, bf16[8192,128]{1,0:T(8,128)(2,1)} %source.1, s32[8,1,1024]{2,1,0:T(1,128)} %bitcast.3, s32[8,1,1024]{2,1,0:T(1,128)} %bitcast.4, bf16[3,3,128,128]{3,2,1,0:T(8,128)(2,1)} %taps.1, f32[1,128]{1,0:T(1,128)} %bitcast.5), custom_call_target="tpu_custom_call" | custom-call | tf_op jit(solution)/shard_map/make_map/pallas_call | solution.py:401
  75.8 1.0 %copy.10 = bf16[16,256,128]{2,1,0:T(8,128)(2,1)} copy(bf16[16,256,128]{2,1,0:T(8,128)(2,1)S(1)} %get-tuple-element.2) | data formatting | bytes 2097152
  76.8 1.0 %copy.11 = bf16[16,256,128]{2,1,0:T(8,128)(2,1)} copy(bf16[16,256,128]{2,1,0:T(8,128)(2,1)S(1)} %get-tuple-element.3) | data formatting | bytes 2097152

commit v3 on v2

--- a/solution.py
+++ b/solution.py
@@ -41,6 +41,8 @@
     send_cells,
     got_feats,
     got_cells,
+    send_map,
+    got_map,
     acc,
     pad,
     edges,
@@ -55,6 +57,8 @@
     own,
     send_h,
     recv_h,
+    send_d,
+    recv_d,
 ):
     devices = size_gx * size_gy
     capacity = send_feats.shape[1]
@@ -65,9 +69,9 @@
 
     @pl.loop(1, devices)
     def _(k):
-        other = lax.rem(me + k, devices)
+        peer = lax.rem(me + k, devices)
         pl.semaphore_signal(
-            barrier, inc=1, device_id=(other // size_gy, lax.rem(other, size_gy)), device_id_type=MESH
+            barrier, inc=1, device_id=(peer // size_gy, lax.rem(peer, size_gy)), device_id_type=MESH
         )
 
     points = (
@@ -143,32 +147,56 @@
             total = part if total is None else total + part
         return total
 
-    def copies(source, owner, target):
+    pairs = devices // 2
+    half = pairs // 2
+    quarter = size_gy // 4
+    upper_me = gy >= size_gy // 2
+
+    def between(y):
+        return (y >= quarter) & (y < size_gy - quarter)
+
+    def mirror(y):
+        return size_gy - 1 - y
+
+    dense = between(gy)
+    other = gx * size_gy + mirror(gy)
+
+    def pair_at(q, sign):
+        i = lax.rem(q, half)
+        far = (q < half) != upper_me
+        col = lax.rem(gx + sign * (i // quarter) + size_gx, size_gx)
+        line = lax.rem(lax.rem(gy // 2, quarter) + sign * lax.rem(i, quarter) + quarter, quarter)
+        return col * (2 * quarter) + jnp.where(far, quarter, 0) + line
+
+    def route(tile):
+        x, y = tile // size_gy, lax.rem(tile, size_gy)
+        relay = between(y) & ((y >= size_gy // 2) != upper_me)
+        target = x * size_gy + jnp.where(relay, mirror(y), y)
+        return target, jnp.where(relay, other, me)
+
+    def copies(source, slot, target):
         where = dict(
             device_id=(target // size_gy, lax.rem(target, size_gy)), device_id_type=MESH
         )
         return (
             pltpu.make_async_remote_copy(
-                send_cells.at[source], got_cells.at[owner],
-                send_c.at[source], recv_c.at[owner], **where,
+                send_cells.at[source], got_cells.at[slot],
+                send_c.at[source], recv_c.at[slot], **where,
             ),
             pltpu.make_async_remote_copy(
-                send_feats.at[source], got_feats.at[owner], send_f.at[source], recv_f.at[owner], **where
+                send_feats.at[source], got_feats.at[slot], send_f.at[source], recv_f.at[slot], **where
             ),
         )
 
-    mine = (
-        pltpu.make_async_copy(send_cells.at[me], got_cells.at[me], own.at[0]),
-        pltpu.make_async_copy(send_feats.at[me], got_feats.at[me], own.at[1]),
-    )
-    pairs = devices // 2
-    half = me // 2
-
-    def offset(q):
-        return lax.rem(2 * q + 1, pairs) - q // (pairs // 2)
+    def mine(slot):
+        at = jnp.where(slot == me, 0, 2)
+        return (
+            pltpu.make_async_copy(send_cells.at[slot], got_cells.at[slot], own.at[at]),
+            pltpu.make_async_copy(send_feats.at[slot], got_feats.at[slot], own.at[at + 1]),
+        )
 
     def pack(q):
-        pair = lax.rem(half + offset(q), pairs)
+        pair = pair_at(q, 1)
         names = [(pair * 2 + k).astype(jnp.float32).astype(jnp.bfloat16) for k in range(2)]
 
         def masked(c):
@@ -181,20 +209,21 @@
         for k in range(2):
             send_feats[pair * 2 + k] = block[:, k * 128 : (k + 1) * 128]
 
-    def send(q, parts=(0, 1)):
-        pair = lax.rem(half + offset(q), pairs)
+    def send(q):
+        pair = pair_at(q, 1)
         for k in range(2):
-            target = pair * 2 + k
+            tile = pair * 2 + k
+            target, slot = route(tile)
 
             @pl.when(target != me)
             def _():
-                for part in parts:
-                    copies(target, me, target)[part].start()
+                for copy in copies(tile, slot, target):
+                    copy.start()
 
             @pl.when(target == me)
             def _():
-                for part in parts:
-                    mine[part].start()
+                for copy in mine(tile):
+                    copy.start()
 
     load.wait()
     pack(jnp.int32(0))
@@ -216,37 +245,38 @@
     pl.semaphore_wait(barrier, devices - 1)
     send(jnp.int32(0))
 
-
-    @pl.loop(1, pairs)
-    def _(q):
+    acc[...] = jnp.zeros_like(acc)
+
+    def advance(q):
         pack(q)
 
         @pl.when(q > 1)
         def _():
             send(q - 1)
 
-    for copy in later:
-        copy.wait()
-    send(jnp.int32(pairs - 1))
-    acc[...] = jnp.zeros_like(acc)
+    turn = half + half // 2
+
+    @pl.loop(1, turn)
+    def _(q):
+        advance(q)
 
     def receive(positions):
         owners = []
         for j in positions:
-            q = lax.rem(j + pairs // 2, pairs)
-            pair = lax.rem(half + pairs - offset(q), pairs)
+            pair = pair_at(j, -1)
             owners += [pair * 2, pair * 2 + 1]
 
         def arrived(part):
             for owner in owners:
-
-                @pl.when(owner != me)
+                local = (owner == me) | (dense & (owner == other))
+
+                @pl.when(jnp.logical_not(local))
                 def _():
                     copies(owner, owner, owner)[part].wait_recv()
 
-                @pl.when(owner == me)
+                @pl.when(local)
                 def _():
-                    mine[part].wait()
+                    mine(owner)[part].wait()
 
         arrived(0)
         row, col = [], []
@@ -274,16 +304,51 @@
 
     group = GROUP // 2
 
-    @pl.loop(0, pairs // group - 1)
-    def _(g):
-        added = receive([g * group + j for j in range(group)])
-        for r in range(0, ROWS_DEV, 2):
-            acc[:, r * 128 : (r + 2) * 128] += added((r, r + 1))
-
-    for j in range(pairs - group, pairs - 1):
-        added = receive([jnp.int32(j)])
-        for r in range(0, ROWS_DEV, 2):
-            acc[:, r * 128 : (r + 2) * 128] += added((r, r + 1))
+    def gather(first):
+        @pl.loop(0, half // group)
+        def _(g):
+            added = receive([first + g * group + j for j in range(group)])
+            for r in range(0, ROWS_DEV, 2):
+                acc[:, r * 128 : (r + 2) * 128] += added((r, r + 1))
+
+    order = [(0, ROWS_DEV - 1)] + [(r, r + 1) for r in range(1, ROWS_DEV - 1, 2)]
+
+    def partial(r):
+        return pltpu.make_async_remote_copy(
+            send_map.at[r], got_map.at[r], send_d.at[r], recv_d.at[r],
+            device_id=(gx, mirror(gy)), device_id_type=MESH,
+        )
+
+    @pl.when(dense)
+    def _():
+        gather(0)
+        before = ()
+        for rows in order:
+            for r in rows:
+                send_map[r] = acc[:, r * 128 : (r + 1) * 128].astype(jnp.bfloat16)
+            for r in before:
+                partial(r).start()
+            before = rows
+        acc[...] = jnp.zeros_like(acc)
+        for r in before:
+            partial(r).start()
+
+    @pl.when(jnp.logical_not(dense))
+    def _():
+        got_map[...] = jnp.zeros_like(got_map)
+
+    @pl.loop(turn, pairs)
+    def _(q):
+        advance(q)
+
+    send(jnp.int32(pairs - 1))
+    for copy in later:
+        copy.wait()
+    gather(half)
+
+    @pl.when(jnp.logical_not(dense))
+    def _():
+        gather(0)
 
     def inside(x, y):
         return (x >= 0) & (x < size_gx) & (y >= 0) & (y < size_gy)
@@ -313,12 +378,14 @@
                 def _():
                     halo(i).start()
 
-    added = receive([jnp.int32(pairs - 1)])
-    order = [(0, ROWS_DEV - 1)] + [(r, r + 1) for r in range(1, ROWS_DEV - 1, 2)]
     for step, rows in enumerate(order):
-        part = added(rows)
-        for k, r in enumerate(rows):
-            total = acc[:, r * 128 : (r + 1) * 128] + part[:, k * 128 : (k + 1) * 128]
+        for r in rows:
+
+            @pl.when(dense)
+            def _():
+                partial(r).wait_recv()
+
+            total = acc[:, r * 128 : (r + 1) * 128] + got_map[r].astype(jnp.float32)
             cells = total.astype(jnp.bfloat16)
             pad[r + 1] = cells
             bev[r] = cells
@@ -380,11 +447,19 @@
         def _():
             halo(i).wait_send()
 
-    @pl.loop(1, devices)
-    def _(k):
-        other = lax.rem(me + k, devices)
-        for copy in copies(other, me, other):
-            copy.wait_send()
+    @pl.when(dense)
+    def _():
+        for r in range(ROWS_DEV):
+            partial(r).wait_send()
+
+    @pl.loop(0, devices)
+    def _(tile):
+        target, slot = route(tile)
+
+        @pl.when(target != me)
+        def _():
+            for copy in copies(tile, slot, target):
+                copy.wait_send()
 
 
 def make_map(count, feats, named, cell, weight, bias, size_gx, size_gy, capacity):
@@ -419,6 +494,8 @@
             pltpu.VMEM((devices, 1, stride), jnp.float32),
             pltpu.VMEM((devices, capacity, channels), jnp.bfloat16),
             pltpu.VMEM((devices, 1, stride), jnp.float32),
+            pltpu.VMEM((ROWS_DEV, COLS_DEV, channels), jnp.bfloat16),
+            pltpu.VMEM((ROWS_DEV, COLS_DEV, channels), jnp.bfloat16),
             pltpu.VMEM((COLS_DEV, ROWS_DEV * channels), jnp.float32),
             pltpu.VMEM((ROWS_DEV + 2, COLS_DEV, channels), jnp.bfloat16),
             pltpu.VMEM((2, ROWS_DEV, 1, channels), jnp.float32),
@@ -430,9 +507,11 @@
             dma((devices,)),
             dma((devices,)),
             dma((devices,)),
-            dma((2,)),
+            dma((4,)),
             dma((len(NEIGHBOURS),)),
             dma((len(NEIGHBOURS),)),
+            dma((ROWS_DEV,)),
+            dma((ROWS_DEV,)),
         ],
         compiler_params=pltpu.CompilerParams(
             collective_id=0, has_side_effects=True, vmem_limit_bytes=36 * 1024 * 1024

time: 77.9 us -> 74.3 us (0.954)
  Pallas kernels: 74.6 us -> 70.9 us
    pallas_call x1, Pallas kernels: 74.6 us -> 70.9 us  [make_map(): pl.pallas_call(functools.partial(map_kernel, size_gx, size_gy), out_shape...]
where the time goes in v3:
time: 74.3 us; the launch traced here: 74.2 us
  Pallas kernels  70.9 us (95%)
  local copies, waits for them, and re-layouts  1.94 us (3%)
  between operations  1.29 us (2%)
    pallas_call x1, Pallas kernels, make_map(): pl.pallas_call(functools.partial(map_kernel, size_gx, size_gy), out_shape...  70.9 us
    unnamed x2, local copies, waits for them, and re-layouts  1.94 us

profile of v3, /device:TPU:0, one launch (start us, length us, event | category | flops | bytes accessed | tf_op | source)
XLA Modules:
  0.0 74.2 jit_solution(9343845147489270064)
XLA Ops:
  1.3 70.9 %make_map.1 = (bf16[16,256,128]{2,1,0:T(8,128)(2,1)S(1)}, bf16[16,256,128]{2,1,0:T(8,128)(2,1)S(1)}) custom-call(s32[1]{0:T(128)S(6)} %copy.12.count, bf16[8192,128]{1,0:T(8,128)(2,1)} %source.1, s32[8,1,1024]{2,1,0:T(1,128)} %bitcast.3, s32[8,1,1024]{2,1,0:T(1,128)} %bitcast.4, bf16[3,3,128,128]{3,2,1,0:T(8,128)(2,1)} %taps.1, f32[1,128]{1,0:T(1,128)} %bitcast.5), custom_call_target="tpu_custom_call" | custom-call | tf_op jit(solution)/shard_map/make_map/pallas_call | solution.py:476
  72.2 1.0 %copy.10 = bf16[16,256,128]{2,1,0:T(8,128)(2,1)} copy(bf16[16,256,128]{2,1,0:T(8,128)(2,1)S(1)} %get-tuple-element.2) | data formatting | bytes 2097152
  73.2 1.0 %copy.11 = bf16[16,256,128]{2,1,0:T(8,128)(2,1)} copy(bf16[16,256,128]{2,1,0:T(8,128)(2,1)S(1)} %get-tuple-element.3) | data formatting | bytes 2097152
